TPU v7x, 32 devices: a whole 2x2x4 slice. The times are simulated.
32 devices in a mesh: mb: 4 (over z), tp: 2 (over y), dp: 4 (over x, core).
Axes of the slice: x: 2, y: 2, z: 4, core: 2. Of those that a mesh axis runs over, the one named last changes fastest.
Arguments:
- hidden: bfloat16 [4, 8, 512, 7168], P('dp', 'mb', None, 'tp'), may hold values from -6 to 6
- latent: bfloat16 [4, 8, 512, 512], P('dp', 'mb', None, 'tp'), may hold values from -6 to 6
- out_grad: bfloat16 [4, 8, 512, 16384], P('dp', 'mb', None, 'tp'), may hold values from -0.059814453 to 0.059814453
- up_weight: bfloat16 [512, 16384], P(None, 'tp'), may hold values from -0.046875 to 0.046875
- mb_tokens: int32 [4, 8], P('dp'), may hold values from 128 to 512, as said below
- slot_mb: int32 [4, 8], P('dp', 'mb'), may hold values from 0 to 7, each once within a row
Outputs:
- up_grad: float32 [512, 16384], P(('mb', 'dp'), 'tp')
- running_down: float32 [4, 7168, 512], P('mb', 'tp', 'dp')
Inputs may be any that keep to these rules, and one draw needn't show every extreme that they name: `mb_tokens`: each count is a multiple of 128; in every group some microbatch has exactly 512 tokens. `slot_mb`: each row is a permutation of the microbatch numbers.
All inputs are finite; a program needn't handle non-finite values.
Results may differ from a plain program's by a relative error of at most 0.005.
Values may be sent and summed in bfloat16 or wider, within the bound.
A program may use at most 128 MiB of HBM per device.

v0:
```python
import functools

import jax
import jax.numpy as jnp
from jax import lax
from jax.experimental import pallas as pl
from jax.experimental.pallas import tpu as pltpu
from jax.sharding import PartitionSpec as P

F32 = jnp.float32
BF16 = jnp.bfloat16
UP_CHUNKS = 8
DOWN_CHUNKS = 7


def bits_of(size):
    count = size.bit_length() - 1
    assert size == 1 << count, "axis size"
    return count


def kernel(sizes, hidden, latent, grad, weight, tokens, slots, up_out, run_out,
           grad_v, weight_v, hidden_v, lat_v, lat_t, lg_acc, lg_send, lg_recv, lg_t,
           up, up_r, dn, dn_r, pre_r, pre_s,
           grad_sem, weight_sem, hidden_sem, lat_sem, lat_ss, lat_rs, lg_ss, lg_rs,
           up_ss, up_rs, dn_ss, dn_rs, pre_ss, pre_rs):
    n_mb, n_tp, n_dp = sizes
    mb, tp, dp = (lax.axis_index(a) for a in ("mb", "tp", "dp"))
    up_chunks, slot_count, cap, width = grad_v.shape
    rows = slot_count * cap
    rank_part = lat_v.shape[-1]
    down_chunks, down_width = dn.shape[0], dn.shape[-1]

    steps = []
    for axis, index, size in (("dp", dp, n_dp), ("mb", mb, n_mb)):
        for k in range(bits_of(size)):
            bit = (index // (1 << k)) % 2
            steps.append((bit, {axis: index + (1 - 2 * bit) * (1 << k)}))
    n_dp_steps = bits_of(n_dp)
    tp_peers = [{"tp": (tp + s) % n_tp} for s in range(1, n_tp)]
    following, preceding = {"mb": (mb + 1) % n_mb}, {"mb": (mb + n_mb - 1) % n_mb}

    def grad_copy(c):
        return pltpu.make_async_copy(
            grad.at[0, :, :, pl.ds(pl.multiple_of(c * width, width), width)], grad_v.at[c], grad_sem.at[c])

    def weight_copy(c):
        return pltpu.make_async_copy(
            weight.at[:, pl.ds(pl.multiple_of(c * width, width), width)], weight_v.at[c % 2], weight_sem.at[c % 2])

    def hidden_copy(c):
        return pltpu.make_async_copy(
            hidden.at[0, :, :, pl.ds(pl.multiple_of(c * down_width, down_width), down_width)],
            hidden_v.at[c % 2], hidden_sem.at[c % 2])

    def remote(src, dst, ss, rs, to):
        return pltpu.make_async_remote_copy(
            src_ref=src, dst_ref=dst, send_sem=ss, recv_sem=rs,
            device_id=to, device_id_type=pl.DeviceIdType.MESH)

    own_latent = pltpu.make_async_copy(latent.at[0], lat_v.at[0], lat_sem)
    own_latent.start()
    for c in range(2):
        weight_copy(c).start()
        hidden_copy(c).start()

    @pl.loop(0, up_chunks)
    def _(c):
        grad_copy(c).start()

    barrier = pltpu.get_barrier_semaphore()
    greeted = [to for _, to in steps] + tp_peers + [following, preceding]
    for to in greeted:
        pl.semaphore_signal(barrier, inc=1, device_id=to, device_id_type=pl.DeviceIdType.MESH)
    pl.semaphore_wait(barrier, len(greeted))

    def lat_copy(s):
        return remote(latent.at[0], lat_v.at[s], lat_ss.at[s - 1], lat_rs.at[s - 1], tp_peers[s - 1])

    def lg_copy(s):
        return remote(lg_send, lg_recv.at[s - 1], lg_ss.at[s - 1], lg_rs.at[s - 1], tp_peers[s - 1])

    for s in range(1, n_tp):
        lat_copy(s).start()

    tp_bits = bits_of(n_tp)
    last = len(steps) - 1
    part_steps = len(steps) - tp_bits

    def part_at(s):
        part = (tp + n_tp - s) % n_tp
        return tuple((part // (1 << k)) % 2 for k in reversed(range(tp_bits)))

    def up_copy(k, s, c):
        bit, to = steps[k]
        head = (c,) + (part_at(s) if k < part_steps else ())
        free = len(steps) - 1 - k - (len(head) - 1)
        src = (up if k == 0 else up_r[k - 1]).at[head + (slice(None),) * free + (1 - bit,)]
        return remote(src, up_r[k].at[head], up_ss.at[k, s, c], up_rs.at[k, s, c], to)

    def up_add(k, s, c):
        bit, _ = steps[k]
        head = (c,) + (part_at(s) if k < part_steps else ())
        free = len(steps) - 1 - k - (len(head) - 1)
        up_copy(k, s, c).wait_recv()
        kept = (up if k == 0 else up_r[k - 1])[head + (slice(None),) * free + (bit,)]
        return kept.astype(F32) + up_r[k][head].astype(F32)

    def up_pass(k, s, c):
        head = (c,) + (part_at(s) if k < part_steps else ())
        up_r[k][head] = up_add(k, s, c).astype(BF16)
        if k + 1 != part_steps:
            up_copy(k + 1, s, c).start()

    def up_make(s, c):
        block = lax.dot_general(
            lat_t[s], grad_v[c].reshape(rows, width),
            (((1,), (0,)), ((), ())), preferred_element_type=F32).astype(BF16)
        head = (c,) + part_at(s)
        up[head] = block.reshape(up.shape[1 + tp_bits:])
        up_copy(0, s, c).start()

    def up_tick(t):
        for k in range(1, last + 1):
            c = t - (k - 1)

            @pl.when((c >= 0) & (c < up_chunks))
            def _():
                if k < part_steps:
                    for s in range(1 if k == 1 else 0, n_tp):
                        up_pass(k, s, c)
                    if k + 1 == part_steps:
                        up_copy(part_steps, 0, c).start()
                elif k < last:
                    up_pass(k, 0, c)
                else:
                    at = pl.ds(pl.multiple_of(c * width, width), width)
                    up_out[:, at] = up_add(k, 0, c)

    def latent_part(s):
        part = lat_v[s].reshape(rows, rank_part).astype(F32)
        part = jnp.where(live(part.shape), part, 0.0)
        lat_t[s] = part.T.astype(BF16)

    def dn_copy(k, c):
        bit, to = steps[k]
        src = (dn if k == 0 else dn_r[k - 1]).at[c]
        index = (slice(None),) * (n_dp_steps - 1 - k) + (1 - bit,)
        return remote(src.at[index], dn_r[k].at[c], dn_ss.at[k, c], dn_rs.at[k, c], to)

    def dn_add(k, c):
        bit, _ = steps[k]
        dn_copy(k, c).wait_recv()
        src = dn if k == 0 else dn_r[k - 1]
        kept = src[(c,) + (slice(None),) * (n_dp_steps - 1 - k) + (bit,)]
        return kept.astype(F32) + dn_r[k][c].astype(F32)

    def dn_pass(k, c):
        dn_r[k][c] = dn_add(k, c).astype(BF16)
        dn_copy(k + 1, c).start()

    def pre_copy(c):
        return remote(pre_s.at[c], pre_r.at[c], pre_ss.at[c], pre_rs.at[c], following)

    counts = [tokens[0, slots[0, s]] for s in range(slot_count)]

    def live(shape):
        row = lax.broadcasted_iota(jnp.int32, shape, 0)
        valid = row < counts[0]
        for s in range(1, slot_count):
            valid = valid | ((row >= s * cap) & (row < s * cap + counts[s]))
        return valid

    own_latent.wait()
    latent_part(0)

    @pl.loop(0, up_chunks)
    def _(c):
        grad_copy(c).wait()
        up_make(0, c)

        @pl.when(c > 0)
        def _():
            up_pass(0, 0, c - 1)

    up_pass(0, 0, up_chunks - 1)

    lg_acc[...] = jnp.zeros_like(lg_acc)

    @pl.loop(0, up_chunks)
    def _(c):
        weight_copy(c).wait()
        lg_acc[...] += lax.dot_general(
            grad_v[c].reshape(rows, width), weight_v[c % 2], (((1,), (1,)), ((), ())),
            preferred_element_type=F32)

        @pl.when(c + 2 < up_chunks)
        def _():
            weight_copy(c + 2).start()

        @pl.when(c > 0)
        def _():
            up_pass(1, 0, c - 1)

    lg_send[...] = lg_acc[...].astype(BF16)
    for s in range(1, n_tp):
        lg_copy(s).start()

    for s in range(1, n_tp):
        lat_copy(s).wait_recv()
        latent_part(s)

        @pl.loop(0, up_chunks)
        def _(c):
            up_make(s, c)

            @pl.when(c > 0)
            def _():
                up_pass(0, s, c - 1)

        up_pass(0, s, up_chunks - 1)

    up_pass(1, 0, up_chunks - 1)
    early = up_chunks - 2

    @pl.loop(0, early)
    def _(t):
        up_tick(t)

    total = lg_acc[...]
    for s in range(1, n_tp):
        lg_copy(s).wait_recv()
        total = total + lg_recv[s - 1].astype(F32)
    total = jnp.where(live(total.shape), total, 0.0)
    lg_t[...] = total.T.astype(BF16)

    @pl.loop(0, down_chunks)
    def _(c):
        hidden_copy(c).wait()
        block = lax.dot_general(
            lg_t[...], hidden_v[c % 2].reshape(rows, down_width),
            (((1,), (0,)), ((), ())), preferred_element_type=F32)
        dn[c] = block.astype(BF16).reshape(dn.shape[1:])
        dn_copy(0, c).start()

        @pl.when(c + 2 < down_chunks)
        def _():
            hidden_copy(c + 2).start()

        @pl.when(c > 0)
        def _():
            dn_pass(0, c - 1)

    dn_pass(0, down_chunks - 1)

    @pl.loop(early, up_chunks + last - 1)
    def _(t):
        up_tick(t)

    for k in range(1, n_dp_steps - 1):
        @pl.loop(0, down_chunks)
        def _(c):
            dn_pass(k, c)

    @pl.loop(0, down_chunks)
    def _(c):
        share = dn_add(n_dp_steps - 1, c)
        at = pl.ds(pl.multiple_of(c * down_width, down_width), down_width)

        @pl.when(mb == 0)
        def _():
            pre_s[c] = share.astype(BF16)
            pre_copy(c).start()
            run_out[0, at, :] = share.T

        @pl.when(mb > 0)
        def _():
            pre_copy(c).wait_recv()
            running = share + pre_r[c].astype(F32)

            @pl.when(mb < n_mb - 1)
            def _():
                pre_s[c] = running.astype(BF16)
                pre_copy(c).start()

            run_out[0, at, :] = running.T

    for s in range(1, n_tp):
        lat_copy(s).wait_send()
        lg_copy(s).wait_send()

    @pl.loop(0, up_chunks)
    def _(c):
        for k in range(len(steps)):
            for s in range(n_tp if k < part_steps else 1):
                up_copy(k, s, c).wait_send()

    @pl.loop(0, down_chunks)
    def _(c):
        for k in range(n_dp_steps):
            dn_copy(k, c).wait_send()

        @pl.when(mb < n_mb - 1)
        def _():
            pre_copy(c).wait_send()


def local(sizes, hidden, latent, out_grad, up_weight, mb_tokens, slot_mb):
    n_mb, n_tp, n_dp = sizes
    _, slot_count, cap, feature_part = hidden.shape
    rank_part = latent.shape[3]
    rank, column_part = up_weight.shape
    rows = slot_count * cap
    width = column_part // UP_CHUNKS
    down_width = feature_part // DOWN_CHUNKS
    dp_bits, mb_bits = bits_of(n_dp), bits_of(n_mb)
    bits = dp_bits + mb_bits
    up_rows = rank >> bits
    share = rank >> dp_bits
    dma = pltpu.SemaphoreType.DMA
    scratch = [
        pltpu.VMEM((UP_CHUNKS, slot_count, cap, width), BF16),
        pltpu.VMEM((2, rank, width), BF16),
        pltpu.VMEM((2, slot_count, cap, down_width), BF16),
        pltpu.VMEM((n_tp, slot_count, cap, rank_part), BF16),
        pltpu.VMEM((n_tp, rank_part, rows), BF16),
        pltpu.VMEM((rows, rank), F32),
        pltpu.VMEM((rows, rank), BF16),
        pltpu.VMEM((n_tp - 1, rows, rank), BF16),
        pltpu.VMEM((rank, rows), BF16),
        pltpu.VMEM((UP_CHUNKS,) + (2,) * bits + (up_rows, width), BF16),
        [pltpu.VMEM((UP_CHUNKS,) + (2,) * (bits - 1 - k) + (up_rows, width), BF16) for k in range(bits)],
        pltpu.VMEM((DOWN_CHUNKS,) + (2,) * dp_bits + (share, down_width), BF16),
        [pltpu.VMEM((DOWN_CHUNKS,) + (2,) * (dp_bits - 1 - k) + (share, down_width), BF16) for k in range(dp_bits)],
        pltpu.VMEM((DOWN_CHUNKS, share, down_width), BF16),
        pltpu.VMEM((DOWN_CHUNKS, share, down_width), BF16),
        dma((UP_CHUNKS,)), dma((2,)), dma((2,)), dma,
        dma((n_tp - 1,)), dma((n_tp - 1,)), dma((n_tp - 1,)), dma((n_tp - 1,)),
        dma((bits, n_tp, UP_CHUNKS)), dma((bits, n_tp, UP_CHUNKS)),
        dma((dp_bits, DOWN_CHUNKS)), dma((dp_bits, DOWN_CHUNKS)),
        dma((DOWN_CHUNKS,)), dma((DOWN_CHUNKS,)),
    ]
    hbm = pl.BlockSpec(memory_space=pl.ANY)
    smem = pl.BlockSpec(memory_space=pltpu.SMEM)
    vmem = pl.BlockSpec(memory_space=pltpu.VMEM)
    return pl.pallas_call(
        functools.partial(kernel, sizes),
        out_shape=(
            jax.ShapeDtypeStruct((up_rows, column_part), F32),
            jax.ShapeDtypeStruct((1, feature_part, share), F32),
        ),
        in_specs=[hbm] * 4 + [smem] * 2,
        out_specs=(vmem, vmem),
        scratch_shapes=scratch,
        compiler_params=pltpu.CompilerParams(
            collective_id=0, has_side_effects=True, vmem_limit_bytes=67043328),
    )(hidden, latent, out_grad, up_weight, mb_tokens, slot_mb)


def solution(mesh):
    sizes = tuple(mesh.shape[axis] for axis in ("mb", "tp", "dp"))
    return jax.shard_map(
        functools.partial(local, sizes),
        mesh=mesh,
        in_specs=(
            P("dp", "mb", None, "tp"),
            P("dp", "mb", None, "tp"),
            P("dp", "mb", None, "tp"),
            P(None, "tp"),
            P("dp", None),
            P("dp", "mb"),
        ),
        out_specs=(P(("mb", "dp"), "tp"), P("mb", "tp", "dp")),
        check_vma=False,
    )
```

profile of v0, /device:TPU:28, one launch (start us, length us, event | category | flops | bytes accessed | tf_op | source)
XLA Modules:
  0.0 118.5 jit_solution(4091809537540323220)
XLA Ops:
  0.6 112.8 %shard_map.77 = (f32[32,8192]{1,0:T(8,128)}, f32[1,3584,128]{2,1,0:T(8,128)}) custom-call(bf16[1,2,512,3584]{3,2,1,0:T(8,128)(2,1)} %hidden.1, bf16[1,2,512,256]{3,2,1,0:T(8,128)(2,1)} %latent.1, bf16[1,2,512,8192]{3,2,1,0:T(8,128)(2,1)} %grad.1, bf16[512,8192]{1,0:T(8,128)(2,1)} %weight.1, s32[1,8]{1,0:T(1,128)} %tokens.1, s32[1,2]{1,0:T(1,128)} %slots.1), custom_call_target="tpu_custom_call" | custom-call | tf_op jit(solution)/shard_map/pallas_call | solution.py:346
  113.4 2.3 %copy.10 = f32[32,8192]{1,0:T(8,128)} copy(f32[32,8192]{1,0:T(8,128)} %get-tuple-element.4) | data formatting | bytes 2097152
  115.7 2.8 %copy.11 = f32[1,3584,128]{2,1,0:T(8,128)} copy(f32[1,3584,128]{2,1,0:T(8,128)} %get-tuple-element.5) | data formatting | bytes 3670016
where the time goes:
time: 119 us
  Pallas kernels  113 us (95%)
  local copies, waits for them, and re-layouts  5.11 us (4%)
    pallas_call x1, Pallas kernels, local(): pl.pallas_call(functools.partial(kernel, sizes), out_shape=(jax.ShapeDtyp...  113 us
    unnamed x2, local copies, waits for them, and re-layouts  5.11 us

commit v1 on v0

v1 whole, which is shorter than its diff:
```python
import functools

import jax
import jax.numpy as jnp
from jax import lax
from jax.experimental import pallas as pl
from jax.experimental.pallas import tpu as pltpu
from jax.sharding import PartitionSpec as P

F32 = jnp.float32
BF16 = jnp.bfloat16
UP_CHUNKS = 8
LATE = 1
LAG = 4
TRAIL = 3


def bits_of(size):
    count = size.bit_length() - 1
    assert size == 1 << count, "axis size"
    return count


def kernel(sizes, hidden, latent, grad, weight, tokens, slots, up_out, run_out,
           grad_v, weight_v, hidden_v, lat_v, lat_t, lg_acc, lg_send, lg_recv, lg_t,
           up, up_r, dn, dn_r, pre_r,
           grad_sem, weight_sem, hidden_sem, lat_sem, lat_ss, lat_rs, lg_ss, lg_rs,
           up_ss, up_rs, dn_ss, dn_rs, pre_ss, pre_rs):
    n_mb, n_tp, n_dp = sizes
    mb, tp, dp = (lax.axis_index(a) for a in ("mb", "tp", "dp"))
    up_chunks, slot_count, cap, width = grad_v.shape
    rows = slot_count * cap
    rank_part = lat_v.shape[-1]
    down_chunks, down_width = dn.shape[0], dn.shape[-1]
    ahead = hidden_v.shape[0]

    dims, partner = [], {}
    for axis, index, size in (("mb", mb, n_mb), ("dp", dp, n_dp)):
        for k in reversed(range(bits_of(size))):
            bit = (index // (1 << k)) % 2
            dims.append((axis, k))
            partner[axis, k] = bit, {axis: index + (1 - 2 * bit) * (1 << k)}
    tp_bits, n_dp_steps = bits_of(n_tp), bits_of(n_dp)
    part_dims = dims[:tp_bits]
    last = len(dims) - 1
    dp_first = dims[::-1]
    mb_first = dp_first[:1] + dp_first[n_dp_steps:] + dp_first[1:n_dp_steps]
    orders = (dp_first, mb_first)
    joints = [min(order.index(d) for d in part_dims) if part_dims else last for order in orders]
    tp_peers = [{"tp": (tp + s) % n_tp} for s in range(1, n_tp)]
    following, preceding = {"mb": (mb + 1) % n_mb}, {"mb": (mb + n_mb - 1) % n_mb}

    def grad_copy(c):
        return pltpu.make_async_copy(
            grad.at[0, :, :, pl.ds(pl.multiple_of(c * width, width), width)], grad_v.at[c], grad_sem.at[c])

    def weight_copy(c):
        return pltpu.make_async_copy(
            weight.at[:, pl.ds(pl.multiple_of(c * width, width), width)], weight_v.at[c], weight_sem.at[c])

    def hidden_copy(c):
        return pltpu.make_async_copy(
            hidden.at[0, :, :, pl.ds(pl.multiple_of(c * down_width, down_width), down_width)],
            hidden_v.at[c % ahead], hidden_sem.at[c % ahead])

    def remote(src, dst, ss, rs, to):
        return pltpu.make_async_remote_copy(
            src_ref=src, dst_ref=dst, send_sem=ss, recv_sem=rs,
            device_id=to, device_id_type=pl.DeviceIdType.MESH)

    barrier = pltpu.get_barrier_semaphore()
    greeted = [to for _, to in partner.values()] + tp_peers + [following, preceding]
    for to in greeted:
        pl.semaphore_signal(barrier, inc=1, device_id=to, device_id_type=pl.DeviceIdType.MESH)

    own_latent = pltpu.make_async_copy(latent.at[0], lat_v.at[0], lat_sem)
    own_latent.start()
    first = up_chunks - LATE
    late = range(first, up_chunks)
    fetched = [c for i in range(LATE) for c in (i, first + i)] + list(range(LATE, first))
    grad_copy(fetched[0]).start()

    counts = [tokens[0, slots[0, s]] for s in range(slot_count)]

    def live(shape):
        row = lax.broadcasted_iota(jnp.int32, shape, 0)
        valid = row < counts[0]
        for s in range(1, slot_count):
            valid = valid | ((row >= s * cap) & (row < s * cap + counts[s]))
        return valid

    def latent_part(s):
        part = lat_v[s].reshape(rows, rank_part).astype(F32)
        part = jnp.where(live(part.shape), part, 0.0)
        lat_t[s] = part.T.astype(BF16)

    own_latent.wait()
    for c in fetched[1:3]:
        grad_copy(c).start()
    latent_part(0)
    pl.semaphore_wait(barrier, len(greeted))

    def lat_copy(s):
        return remote(lat_v.at[0], lat_v.at[s], lat_ss.at[s - 1], lat_rs.at[s - 1], tp_peers[s - 1])

    def lg_copy(s, slot):
        return remote(lg_send.at[slot], lg_recv.at[s - 1, slot],
                      lg_ss.at[s - 1, slot], lg_rs.at[s - 1, slot], tp_peers[s - 1])

    for s in range(1, n_tp):
        lat_copy(s).start()
    for c in fetched[3:]:
        grad_copy(c).start()
    for c in range(up_chunks):
        weight_copy(c).start()
    for c in range(ahead):
        hidden_copy(c).start()

    def part_at(s):
        part = (tp + n_tp - s) % n_tp
        return {d: (part // (1 << k)) % 2 for k, d in enumerate(reversed(part_dims))}

    def up_refs(o, k, s, c, side):
        step = orders[o][k]
        bit, to = partner[step]
        fixed = part_at(s) if k < joints[o] else {}
        taken = {**fixed, step: (1 - bit) if side else bit}
        before = [d for d in dims if d not in orders[o][:k]]
        after = [d for d in before if d != step]
        src = (up if k == 0 else up_r[k - 1], (c,) + tuple(taken.get(d, slice(None)) for d in before))
        dst = (up_r[k], (c,) + tuple(fixed.get(d, slice(None)) for d in after))
        return src, dst, to

    def up_copy(o, k, s, c):
        (src, at), (dst, to_at), to = up_refs(o, k, s, c, 1)
        return remote(src.at[at], dst.at[to_at], up_ss.at[k, s, c], up_rs.at[k, s, c], to)

    def up_add(o, k, s, c):
        (src, at), (dst, to_at), _ = up_refs(o, k, s, c, 0)
        up_copy(o, k, s, c).wait_recv()
        return src[at].astype(F32) + dst[to_at].astype(F32)

    def up_pass(o, k, s, c):
        _, (dst, to_at), _ = up_refs(o, k, s, c, 0)
        dst[to_at] = up_add(o, k, s, c).astype(BF16)
        if k + 1 != joints[o]:
            up_copy(o, k + 1, s, c).start()

    def up_make(s, c):
        block = lax.dot_general(
            lat_t[s], grad_v[c].reshape(rows, width),
            (((1,), (0,)), ((), ())), preferred_element_type=F32).astype(BF16)
        fixed = part_at(s)
        head = tuple(fixed[d] for d in part_dims)
        up[(c,) + head] = block.reshape(up.shape[1 + tp_bits:])
        up_copy(0, 0, s, c).start()

    def up_deep(o, s, c, k):
        for j in range(k, joints[o]):
            up_pass(o, j, s, c)

    def up_finish(o, c):
        for j in range(joints[o], last):
            up_pass(o, j, 0, c)
        up_write(o, c)

    def up_write(o, c):
        at = pl.ds(pl.multiple_of(c * width, width), width)
        up_out[:, at] = up_add(o, last, 0, c)

    others = range(1, n_tp)

    def up_second(c):
        for s in others:
            up_pass(0, 1, s, c)

    def up_join(c):
        for s in others:
            up_deep(0, s, c, 2)
        up_copy(0, joints[0], 0, c).start()

    def dn_copy(k, c):
        bit, to = partner["dp", k]
        src = (dn if k == 0 else dn_r[k - 1]).at[c]
        index = (slice(None),) * (n_dp_steps - 1 - k) + (1 - bit,)
        return remote(src.at[index], dn_r[k].at[c], dn_ss.at[k, c], dn_rs.at[k, c], to)

    def dn_add(k, c):
        bit, _ = partner["dp", k]
        dn_copy(k, c).wait_recv()
        src = dn if k == 0 else dn_r[k - 1]
        kept = src[(c,) + (slice(None),) * (n_dp_steps - 1 - k) + (bit,)]
        return kept.astype(F32) + dn_r[k][c].astype(F32)

    def dn_pass(k, c):
        dn_r[k][c] = dn_add(k, c).astype(BF16)
        dn_copy(k + 1, c).start()

    def pre_copy(c):
        return remote(dn.at[pre_at(c)], pre_r.at[c], pre_ss.at[c], pre_rs.at[c], following)

    def pre_at(c):
        return (c,) + (0,) * (n_dp_steps - 1) + (partner["dp", 0][0],)

    def run_at(c):
        return pl.ds(pl.multiple_of(c * down_width, down_width), down_width)

    def dn_share(c):
        for k in range(1, n_dp_steps - 1):
            dn_pass(k, c)
        share = dn_add(n_dp_steps - 1, c)

        run_out[0, run_at(c), :] = share.T

        @pl.when(mb == 0)
        def _():
            dn[pre_at(c)] = share.astype(BF16)
            pre_copy(c).start()

    def prefix(c):
        @pl.when((mb > 0) & (c >= 0) & (c < down_chunks))
        def _():
            pre_copy(c).wait_recv()
            running = run_out[0, run_at(c), :] + pre_r[c].astype(F32).T
            run_out[0, run_at(c), :] = running

            @pl.when(mb < n_mb - 1)
            def _():
                dn[pre_at(c)] = running.T.astype(BF16)
                pre_copy(c).start()

    def lg_step(slot, j):
        total = lg_acc[slot]
        for c in (2 * j, 2 * j + 1):
            total = total + lax.dot_general(
                weight_v[c], grad_v[c, slot], (((1,), (1,)), ((), ())), preferred_element_type=F32)
        lg_acc[slot] = total

    def lg_start(slot):
        lg_send[slot] = lg_acc[slot].astype(BF16)
        for s in others:
            lg_copy(s, slot).start()

    pairs = up_chunks // 2
    lg_acc[...] = jnp.zeros_like(lg_acc)

    @pl.loop(0, LATE)
    def _(i):
        for c in (i, first + i):
            grad_copy(c).wait()
            up_make(0, c)

        @pl.when(i >= 1)
        def _():
            up_pass(0, 0, 0, i - 1)
            up_pass(1, 0, 0, first + i - 1)

    @pl.loop(LATE, first)
    def _(c):
        grad_copy(c).wait()
        up_make(0, c)

        @pl.when(c == LATE)
        def _():
            up_pass(0, 0, 0, LATE - 1)

        @pl.when(c == LATE + 1)
        def _():
            up_pass(1, 0, 0, up_chunks - 1)

        @pl.when(c >= LATE + 2)
        def _():
            up_pass(0, 0, 0, c - 2)

    @pl.loop(0, pairs)
    def _(j):
        for c in (2 * j, 2 * j + 1):
            weight_copy(c).wait()
        lg_step(0, j)

        @pl.when(j < 2)
        def _():
            up_pass(0, 0, 0, first - 2 + j)

        @pl.when(j % 2 == 1)
        def _():
            up_pass(0, 1, 0, j // 2)

    lg_start(0)

    for s in others:
        lat_copy(s).wait_recv()
        latent_part(s)
        for c in late:
            up_make(s, c)

    for slot in range(1, slot_count):
        @pl.loop(0, pairs)
        def _(j):
            lg_step(slot, j)
            if slot == 1:
                @pl.when(j == 0)
                def _():
                    for s in others:
                        for c in late:
                            up_pass(1, 0, s, c)
                    up_pass(0, 1, 0, 2)

                @pl.when(j % 2 == 1)
                def _():
                    up_deep(0, 0, j // 2, 2)

        lg_start(slot)
    up_pass(0, 1, 0, 3)

    for s in others:
        @pl.loop(0, first)
        def _(c):
            up_make(s, c)

            @pl.when(c >= 2)
            def _():
                up_pass(0, 0, s, c - 2)

            if s == 1:
                @pl.when((c == 2) | (c == 6))
                def _():
                    up_pass(0, 1, 0, 4 + c // 4)

        for c in range(first - 2, first):
            up_pass(0, 0, s, c)

    up_deep(0, 0, 2, 2)
    up_deep(0, 0, 3, 2)
    for c in range(6, first):
        up_pass(0, 1, 0, c)
    for c in late:
        for s in range(n_tp):
            up_deep(1, s, c, 1)
        up_copy(1, joints[1], 0, c).start()
    up_deep(0, 0, 4, 2)
    up_second(0)
    up_deep(0, 0, 5, 2)
    up_second(1)
    for c in range(6, first):
        up_deep(0, 0, c, 2)
    up_join(0)
    up_second(2)
    up_join(1)

    for slot in range(slot_count):
        total = lg_acc[slot]
        for s in others:
            lg_copy(s, slot).wait_recv()
            total = total + lg_recv[s - 1, slot].astype(F32)
        token = lax.broadcasted_iota(jnp.int32, total.shape, 1)
        total = jnp.where(token < counts[slot], total, 0.0)
        lg_t[:, slot * cap:(slot + 1) * cap] = total.astype(BF16)

    @pl.loop(0, down_chunks)
    def _(c):
        hidden_copy(c).wait()
        block = lax.dot_general(
            lg_t[...], hidden_v[c % ahead].reshape(rows, down_width),
            (((1,), (0,)), ((), ())), preferred_element_type=F32)
        dn[c] = block.astype(BF16).reshape(dn.shape[1:])
        dn_copy(0, c).start()

        @pl.when(c + ahead < down_chunks)
        def _():
            hidden_copy(c + ahead).start()

        @pl.when(c >= TRAIL)
        def _():
            dn_pass(0, c - TRAIL)

        for n, at in enumerate((2, 4, 6)):
            @pl.when(c == down_chunks * at // 7)
            def _():
                up_second(3 + n)
                up_join(2 + n)

    for c in range(down_chunks - TRAIL, down_chunks):
        dn_pass(0, c)
    for c in late:
        up_pass(1, joints[1], 0, c)
    for c in range(6, first):
        up_second(c)
        up_join(c - 1)

    @pl.loop(0, down_chunks)
    def _(t):
        dn_share(t)

        @pl.when(t == 2)
        def _():
            up_join(first - 1)

        prefix(t - LAG * mb)

    @pl.loop(0, first)
    def _(c):
        up_finish(0, c)

    for c in late:
        for j in range(joints[1] + 1, last):
            up_pass(1, j, 0, c)
        up_write(1, c)

    @pl.loop(0, LAG * (n_mb - 1))
    def _(u):
        prefix(down_chunks + u - LAG * mb)

    for s in others:
        lat_copy(s).wait_send()
        for slot in range(slot_count):
            lg_copy(s, slot).wait_send()

    def up_sent(o, c):
        for k in range(last + 1):
            for s in range(n_tp if k < joints[o] else 1):
                up_copy(o, k, s, c).wait_send()

    @pl.loop(0, first)
    def _(c):
        up_sent(0, c)

    for c in late:
        up_sent(1, c)

    @pl.loop(0, down_chunks)
    def _(c):
        for k in range(n_dp_steps):
            dn_copy(k, c).wait_send()

        @pl.when(mb < n_mb - 1)
        def _():
            pre_copy(c).wait_send()


def local(sizes, hidden, latent, out_grad, up_weight, mb_tokens, slot_mb):
    n_mb, n_tp, n_dp = sizes
    _, slot_count, cap, feature_part = hidden.shape
    rank_part = latent.shape[3]
    rank, column_part = up_weight.shape
    rows = slot_count * cap
    width = column_part // UP_CHUNKS
    down_chunks = next(n for n in (14, 7) if feature_part % (128 * n) == 0)
    down_width = feature_part // down_chunks
    ahead = 2 * down_chunks // 7
    dp_bits, mb_bits = bits_of(n_dp), bits_of(n_mb)
    bits = dp_bits + mb_bits
    up_rows = rank >> bits
    share = rank >> dp_bits
    dma = pltpu.SemaphoreType.DMA
    scratch = [
        pltpu.VMEM((UP_CHUNKS, slot_count, cap, width), BF16),
        pltpu.VMEM((UP_CHUNKS, rank, width), BF16),
        pltpu.VMEM((ahead, slot_count, cap, down_width), BF16),
        pltpu.VMEM((n_tp, slot_count, cap, rank_part), BF16),
        pltpu.VMEM((n_tp, rank_part, rows), BF16),
        pltpu.VMEM((slot_count, rank, cap), F32),
        pltpu.VMEM((slot_count, rank, cap), BF16),
        pltpu.VMEM((n_tp - 1, slot_count, rank, cap), BF16),
        pltpu.VMEM((rank, rows), BF16),
        pltpu.VMEM((UP_CHUNKS,) + (2,) * bits + (up_rows, width), BF16),
        [pltpu.VMEM((UP_CHUNKS,) + (2,) * (bits - 1 - k) + (up_rows, width), BF16) for k in range(bits)],
        pltpu.VMEM((down_chunks,) + (2,) * dp_bits + (share, down_width), BF16),
        [pltpu.VMEM((down_chunks,) + (2,) * (dp_bits - 1 - k) + (share, down_width), BF16) for k in range(dp_bits)],
        pltpu.VMEM((down_chunks, share, down_width), BF16),
        dma((UP_CHUNKS,)), dma((UP_CHUNKS,)), dma((ahead,)), dma,
        dma((n_tp - 1,)), dma((n_tp - 1,)), dma((n_tp - 1, slot_count)), dma((n_tp - 1, slot_count)),
        dma((bits, n_tp, UP_CHUNKS)), dma((bits, n_tp, UP_CHUNKS)),
        dma((dp_bits, down_chunks)), dma((dp_bits, down_chunks)),
        dma((down_chunks,)), dma((down_chunks,)),
    ]
    hbm = pl.BlockSpec(memory_space=pl.ANY)
    smem = pl.BlockSpec(memory_space=pltpu.SMEM)
    vmem = pl.BlockSpec(memory_space=pltpu.VMEM)
    return pl.pallas_call(
        functools.partial(kernel, sizes),
        out_shape=(
            jax.ShapeDtypeStruct((up_rows, column_part), F32),
            jax.ShapeDtypeStruct((1, feature_part, share), F32),
        ),
        in_specs=[hbm] * 4 + [smem] * 2,
        out_specs=(vmem, vmem),
        scratch_shapes=scratch,
        compiler_params=pltpu.CompilerParams(
            collective_id=0, has_side_effects=True, vmem_limit_bytes=67043328),
    )(hidden, latent, out_grad, up_weight, mb_tokens, slot_mb)


def solution(mesh):
    sizes = tuple(mesh.shape[axis] for axis in ("mb", "tp", "dp"))
    return jax.shard_map(
        functools.partial(local, sizes),
        mesh=mesh,
        in_specs=(
            P("dp", "mb", None, "tp"),
            P("dp", "mb", None, "tp"),
            P("dp", "mb", None, "tp"),
            P(None, "tp"),
            P("dp", None),
            P("dp", "mb"),
        ),
        out_specs=(P(("mb", "dp"), "tp"), P("mb", "tp", "dp")),
        check_vma=False,
    )
```

time: 119 us -> 95.2 us (0.80)
  Pallas kernels: 113 us -> 89.3 us
    pallas_call x1, Pallas kernels: 113 us -> 89.3 us  [local(): pl.pallas_call(functools.partial(kernel, sizes), out_shape=(jax.ShapeDtyp...]
where the time goes in v1:
time: 95.2 us; the launch traced here: 95 us
  Pallas kernels  89.3 us (94%)
  local copies, waits for them, and re-layouts  5.11 us (5%)
    pallas_call x1, Pallas kernels, local(): pl.pallas_call(functools.partial(kernel, sizes), out_shape=(jax.ShapeDtyp...  89.3 us
    unnamed x2, local copies, waits for them, and re-layouts  5.11 us

profile of v1, /device:TPU:28, one launch (start us, length us, event | category | flops | bytes accessed | tf_op | source)
XLA Modules:
  0.0 95.0 jit_solution(17544662620705204195)
XLA Ops:
  0.6 89.3 %shard_map.77 = (f32[32,8192]{1,0:T(8,128)}, f32[1,3584,128]{2,1,0:T(8,128)}) custom-call(bf16[1,2,512,3584]{3,2,1,0:T(8,128)(2,1)} %hidden.1, bf16[1,2,512,256]{3,2,1,0:T(8,128)(2,1)} %latent.1, bf16[1,2,512,8192]{3,2,1,0:T(8,128)(2,1)} %grad.1, bf16[512,8192]{1,0:T(8,128)(2,1)} %weight.1, s32[1,8]{1,0:T(1,128)} %tokens.1, s32[1,2]{1,0:T(1,128)} %slots.1), custom_call_target="tpu_custom_call" | custom-call | tf_op jit(solution)/shard_map/pallas_call | solution.py:480
  89.9 2.3 %copy.10 = f32[32,8192]{1,0:T(8,128)} copy(f32[32,8192]{1,0:T(8,128)} %get-tuple-element.4) | data formatting | bytes 2097152
  92.2 2.8 %copy.11 = f32[1,3584,128]{2,1,0:T(8,128)} copy(f32[1,3584,128]{2,1,0:T(8,128)} %get-tuple-element.5) | data formatting | bytes 3670016

commit v2 on v1

--- a/solution.py
+++ b/solution.py
@@ -10,9 +10,10 @@
 F32 = jnp.float32
 BF16 = jnp.bfloat16
 UP_CHUNKS = 8
-LATE = 1
+LATE = 2
+EARLY = 4
 LAG = 4
-TRAIL = 3
+TRAIL = 2
 
 
 def bits_of(size):
@@ -77,7 +78,7 @@
     own_latent.start()
     first = up_chunks - LATE
     late = range(first, up_chunks)
-    fetched = [c for i in range(LATE) for c in (i, first + i)] + list(range(LATE, first))
+    fetched = [0, late[0], 1, *late[1:], *range(2, first)]
     grad_copy(fetched[0]).start()
 
     counts = [tokens[0, slots[0, s]] for s in range(slot_count)]
@@ -135,14 +136,15 @@
         (src, at), (dst, to_at), to = up_refs(o, k, s, c, 1)
         return remote(src.at[at], dst.at[to_at], up_ss.at[k, s, c], up_rs.at[k, s, c], to)
 
-    def up_add(o, k, s, c):
+    def up_add(o, k, s, c, waited=False):
         (src, at), (dst, to_at), _ = up_refs(o, k, s, c, 0)
-        up_copy(o, k, s, c).wait_recv()
+        if not waited:
+            up_copy(o, k, s, c).wait_recv()
         return src[at].astype(F32) + dst[to_at].astype(F32)
 
-    def up_pass(o, k, s, c):
+    def up_pass(o, k, s, c, waited=False):
         _, (dst, to_at), _ = up_refs(o, k, s, c, 0)
-        dst[to_at] = up_add(o, k, s, c).astype(BF16)
+        dst[to_at] = up_add(o, k, s, c, waited).astype(BF16)
         if k + 1 != joints[o]:
             up_copy(o, k + 1, s, c).start()
 
@@ -159,14 +161,14 @@
         for j in range(k, joints[o]):
             up_pass(o, j, s, c)
 
-    def up_finish(o, c):
+    def up_finish(o, c, waited=False):
         for j in range(joints[o], last):
-            up_pass(o, j, 0, c)
-        up_write(o, c)
-
-    def up_write(o, c):
+            up_pass(o, j, 0, c, waited and j == joints[o])
+        up_write(o, c, waited and joints[o] == last)
+
+    def up_write(o, c, waited=False):
         at = pl.ds(pl.multiple_of(c * width, width), width)
-        up_out[:, at] = up_add(o, last, 0, c)
+        up_out[:, at] = up_add(o, last, 0, c, waited)
 
     others = range(1, n_tp)
 
@@ -249,38 +251,36 @@
         for c in (i, first + i):
             grad_copy(c).wait()
             up_make(0, c)
-
-        @pl.when(i >= 1)
-        def _():
-            up_pass(0, 0, 0, i - 1)
+        up_pass(0, 0, 0, i)
+
+        @pl.when(i > 0)
+        def _():
             up_pass(1, 0, 0, first + i - 1)
 
-    @pl.loop(LATE, first)
+    @pl.loop(LATE, EARLY)
     def _(c):
         grad_copy(c).wait()
         up_make(0, c)
 
         @pl.when(c == LATE)
         def _():
-            up_pass(0, 0, 0, LATE - 1)
-
-        @pl.when(c == LATE + 1)
-        def _():
             up_pass(1, 0, 0, up_chunks - 1)
-
-        @pl.when(c >= LATE + 2)
-        def _():
-            up_pass(0, 0, 0, c - 2)
 
     @pl.loop(0, pairs)
     def _(j):
         for c in (2 * j, 2 * j + 1):
             weight_copy(c).wait()
+
+        @pl.when(2 * j == EARLY)
+        def _():
+            for c in range(EARLY, first):
+                grad_copy(c).wait()
+
         lg_step(0, j)
 
         @pl.when(j < 2)
         def _():
-            up_pass(0, 0, 0, first - 2 + j)
+            up_pass(0, 0, 0, 2 + j)
 
         @pl.when(j % 2 == 1)
         def _():
@@ -288,65 +288,75 @@
 
     lg_start(0)
 
+    @pl.loop(EARLY, first)
+    def _(c):
+        up_make(0, c)
+
+    up_pass(0, 0, 0, EARLY)
     for s in others:
         lat_copy(s).wait_recv()
         latent_part(s)
-        for c in late:
+        @pl.loop(0, LATE)
+        def _(i):
+            up_make(s, first + i)
+
+        @pl.loop(0, EARLY)
+        def _(c):
             up_make(s, c)
+
+            @pl.when(c < LATE)
+            def _():
+                up_pass(1, 0, s, first + c)
+
+            @pl.when(c >= 2)
+            def _():
+                up_pass(0, 0, s, c - 2)
+
+        if s == 1:
+            up_pass(0, 1, 0, 2)
 
     for slot in range(1, slot_count):
         @pl.loop(0, pairs)
         def _(j):
             lg_step(slot, j)
             if slot == 1:
-                @pl.when(j == 0)
+                @pl.when(j < 2)
                 def _():
                     for s in others:
-                        for c in late:
-                            up_pass(1, 0, s, c)
-                    up_pass(0, 1, 0, 2)
+                        up_pass(0, 0, s, 2 + j)
+
+                @pl.when(j % 2 == 0)
+                def _():
+                    up_pass(0, 1, 0, 3 + j // 2)
 
                 @pl.when(j % 2 == 1)
                 def _():
                     up_deep(0, 0, j // 2, 2)
 
         lg_start(slot)
-    up_pass(0, 1, 0, 3)
-
+
+    for c in range(EARLY + 1, first):
+        up_pass(0, 0, 0, c)
+    up_second(0)
     for s in others:
-        @pl.loop(0, first)
+        @pl.loop(EARLY, first)
         def _(c):
             up_make(s, c)
 
-            @pl.when(c >= 2)
-            def _():
-                up_pass(0, 0, s, c - 2)
-
-            if s == 1:
-                @pl.when((c == 2) | (c == 6))
-                def _():
-                    up_pass(0, 1, 0, 4 + c // 4)
-
-        for c in range(first - 2, first):
+        for c in range(EARLY, first):
             up_pass(0, 0, s, c)
-
     up_deep(0, 0, 2, 2)
-    up_deep(0, 0, 3, 2)
-    for c in range(6, first):
-        up_pass(0, 1, 0, c)
+    up_second(1)
     for c in late:
         for s in range(n_tp):
             up_deep(1, s, c, 1)
         up_copy(1, joints[1], 0, c).start()
-    up_deep(0, 0, 4, 2)
-    up_second(0)
-    up_deep(0, 0, 5, 2)
-    up_second(1)
-    for c in range(6, first):
-        up_deep(0, 0, c, 2)
+    up_second(2)
+    up_deep(0, 0, 3, 2)
     up_join(0)
-    up_second(2)
+    up_second(3)
     up_join(1)
+    up_pass(0, 1, 0, 5)
 
     for slot in range(slot_count):
         total = lg_acc[slot]
@@ -374,42 +384,74 @@
         def _():
             dn_pass(0, c - TRAIL)
 
-        for n, at in enumerate((2, 4, 6)):
-            @pl.when(c == down_chunks * at // 7)
-            def _():
-                up_second(3 + n)
-                up_join(2 + n)
+        @pl.when(c == down_chunks * 2 // 7)
+        def _():
+            up_second(4)
+            up_join(2)
+
+        @pl.when(c == down_chunks * 4 // 7)
+        def _():
+            up_deep(0, 0, 4, 2)
+            up_join(3)
+
+        @pl.when(c == down_chunks * 5 // 7)
+        def _():
+            up_second(5)
+            dn_share(0)
+
+        @pl.when(c == down_chunks * 6 // 7)
+        def _():
+            dn_share(1)
 
     for c in range(down_chunks - TRAIL, down_chunks):
         dn_pass(0, c)
     for c in late:
         up_pass(1, joints[1], 0, c)
-    for c in range(6, first):
-        up_second(c)
-        up_join(c - 1)
-
-    @pl.loop(0, down_chunks)
+
+    @pl.loop(2, down_chunks)
     def _(t):
         dn_share(t)
 
-        @pl.when(t == 2)
-        def _():
-            up_join(first - 1)
-
         prefix(t - LAG * mb)
 
-    @pl.loop(0, first)
+    held = (first - 2, first - 1)
+    high = partner[orders[0][joints[0]]][0] == 1
+
+    @pl.loop(0, LAG * (n_mb - 1))
+    def _(u):
+        @pl.when(high & (u == 2 * mb))
+        def _():
+            up_deep(0, 0, held[-1], 2)
+            for c in held:
+                up_join(c)
+
+        prefix(down_chunks + u - LAG * mb)
+
+    @pl.when(jnp.logical_not(high))
+    def _():
+        up_deep(0, 0, held[-1], 2)
+        for c in held:
+            for s in others:
+                up_deep(0, s, c, 2)
+            up_copy(0, joints[0], 0, c).wait_recv()
+            up_copy(0, joints[0], 0, c).start()
+
+    @pl.when(high)
+    def _():
+        for c in held:
+            up_copy(0, joints[0], 0, c).wait_recv()
+
+    @pl.loop(0, first - len(held))
     def _(c):
         up_finish(0, c)
+
+    for c in held:
+        up_finish(0, c, True)
 
     for c in late:
         for j in range(joints[1] + 1, last):
             up_pass(1, j, 0, c)
         up_write(1, c)
-
-    @pl.loop(0, LAG * (n_mb - 1))
-    def _(u):
-        prefix(down_chunks + u - LAG * mb)
 
     for s in others:
         lat_copy(s).wait_send()
@@ -480,14 +522,14 @@
     return pl.pallas_call(
         functools.partial(kernel, sizes),
         out_shape=(
-            jax.ShapeDtypeStruct((up_rows, column_part), F32),
-            jax.ShapeDtypeStruct((1, feature_part, share), F32),
+            pltpu.VMEM((up_rows, column_part), F32),
+            pltpu.VMEM((1, feature_part, share), F32),
         ),
         in_specs=[hbm] * 4 + [smem] * 2,
         out_specs=(vmem, vmem),
         scratch_shapes=scratch,
         compiler_params=pltpu.CompilerParams(
-            collective_id=0, has_side_effects=True, vmem_limit_bytes=67043328),
+            collective_id=0, has_side_effects=True, vmem_limit_bytes=63700992),
     )(hidden, latent, out_grad, up_weight, mb_tokens, slot_mb)
 
 

time: 95.2 us -> 87.3 us (0.917)
  Pallas kernels: 89.3 us -> 83.9 us
  local copies, waits for them, and re-layouts: 5.11 us -> 2.2 us
    pallas_call x1, Pallas kernels: 89.3 us -> 83.9 us  [local(): pl.pallas_call(functools.partial(kernel, sizes), out_shape=(pltpu.VMEM((u...]
    unnamed x2, local copies, waits for them, and re-layouts: 5.11 us -> 2.2 us
where the time goes in v2:
time: 87.3 us; the launch traced here: 86.7 us
  Pallas kernels  83.9 us (96%)
  local copies, waits for them, and re-layouts  2.2 us (3%)
    pallas_call x1, Pallas kernels, local(): pl.pallas_call(functools.partial(kernel, sizes), out_shape=(pltpu.VMEM((u...  83.9 us
    unnamed x2, local copies, waits for them, and re-layouts  2.2 us

profile of v2, /device:TPU:28, one launch (start us, length us, event | category | flops | bytes accessed | tf_op | source)
XLA Modules:
  0.0 86.7 jit_solution(1917029703794141521)
XLA Ops:
  0.6 83.9 %shard_map.77 = (f32[32,8192]{1,0:T(8,128)S(1)}, f32[1,3584,128]{2,1,0:T(8,128)S(1)}) custom-call(bf16[1,2,512,3584]{3,2,1,0:T(8,128)(2,1)} %hidden.1, bf16[1,2,512,256]{3,2,1,0:T(8,128)(2,1)} %latent.1, bf16[1,2,512,8192]{3,2,1,0:T(8,128)(2,1)} %grad.1, bf16[512,8192]{1,0:T(8,128)(2,1)} %weight.1, s32[1,8]{1,0:T(1,128)} %tokens.1, s32[1,2]{1,0:T(1,128)} %slots.1), custom_call_target="tpu_custom_call" | custom-call | tf_op jit(solution)/shard_map/pallas_call | solution.py:522
  84.5 1.0 %copy.10 = f32[32,8192]{1,0:T(8,128)} copy(f32[32,8192]{1,0:T(8,128)S(1)} %get-tuple-element.2) | data formatting | bytes 2097152
  85.5 1.2 %copy.11 = f32[1,3584,128]{2,1,0:T(8,128)} copy(f32[1,3584,128]{2,1,0:T(8,128)S(1)} %get-tuple-element.3) | data formatting | bytes 3670016

commit v3 on v2

--- a/solution.py
+++ b/solution.py
@@ -14,6 +14,7 @@
 EARLY = 4
 LAG = 4
 TRAIL = 2
+SENT = 8
 
 
 def bits_of(size):
@@ -78,7 +79,7 @@
     own_latent.start()
     first = up_chunks - LATE
     late = range(first, up_chunks)
-    fetched = [0, late[0], 1, *late[1:], *range(2, first)]
+    fetched = [c for i in range(LATE) for c in (first + i, i)] + list(range(LATE, first))
     grad_copy(fetched[0]).start()
 
     counts = [tokens[0, slots[0, s]] for s in range(slot_count)]
@@ -198,8 +199,16 @@
         dn_r[k][c] = dn_add(k, c).astype(BF16)
         dn_copy(k + 1, c).start()
 
-    def pre_copy(c):
-        return remote(dn.at[pre_at(c)], pre_r.at[c], pre_ss.at[c], pre_rs.at[c], following)
+    halves = pre_ss.shape[1]
+    half = down_width // halves
+
+    def pre_copy(c, h):
+        at = slice(None), pl.ds(h * half, half)
+        return remote(dn.at[pre_at(c) + at], pre_r.at[(c,) + at], pre_ss.at[c, h], pre_rs.at[c, h], following)
+
+    def pre_sent(c):
+        for h in range(halves):
+            pre_copy(c, h).wait_send()
 
     def pre_at(c):
         return (c,) + (0,) * (n_dp_steps - 1) + (partner["dp", 0][0],)
@@ -217,19 +226,27 @@
         @pl.when(mb == 0)
         def _():
             dn[pre_at(c)] = share.astype(BF16)
-            pre_copy(c).start()
+            for h in range(halves):
+                pre_copy(c, h).start()
 
     def prefix(c):
+        @pl.when((mb < n_mb - 1) & (c >= SENT) & (c < down_chunks + SENT))
+        def _():
+            pre_sent(c - SENT)
+
         @pl.when((mb > 0) & (c >= 0) & (c < down_chunks))
         def _():
-            pre_copy(c).wait_recv()
-            running = run_out[0, run_at(c), :] + pre_r[c].astype(F32).T
-            run_out[0, run_at(c), :] = running
-
-            @pl.when(mb < n_mb - 1)
-            def _():
-                dn[pre_at(c)] = running.T.astype(BF16)
-                pre_copy(c).start()
+            for h in range(halves):
+                cols = pl.ds(h * half, half)
+                rows_at = pl.ds(pl.multiple_of(c * down_width + h * half, half), half)
+                pre_copy(c, h).wait_recv()
+                running = run_out[0, rows_at, :] + pre_r[c, :, cols].astype(F32).T
+                run_out[0, rows_at, :] = running
+
+                @pl.when(mb < n_mb - 1)
+                def _():
+                    dn[pre_at(c) + (slice(None), cols)] = running.T.astype(BF16)
+                    pre_copy(c, h).start()
 
     def lg_step(slot, j):
         total = lg_acc[slot]
@@ -248,14 +265,16 @@
 
     @pl.loop(0, LATE)
     def _(i):
-        for c in (i, first + i):
-            grad_copy(c).wait()
-            up_make(0, c)
-        up_pass(0, 0, 0, i)
+        grad_copy(first + i).wait()
+        up_make(0, first + i)
 
         @pl.when(i > 0)
         def _():
-            up_pass(1, 0, 0, first + i - 1)
+            up_pass(0, 0, 0, i - 1)
+
+        grad_copy(i).wait()
+        up_make(0, i)
+        up_pass(1, 0, 0, first + i)
 
     @pl.loop(LATE, EARLY)
     def _(c):
@@ -264,7 +283,7 @@
 
         @pl.when(c == LATE)
         def _():
-            up_pass(1, 0, 0, up_chunks - 1)
+            up_pass(0, 0, 0, LATE - 1)
 
     @pl.loop(0, pairs)
     def _(j):
@@ -300,6 +319,9 @@
         def _(i):
             up_make(s, first + i)
 
+        if s == 1:
+            up_pass(0, 1, 0, 2)
+
         @pl.loop(0, EARLY)
         def _(c):
             up_make(s, c)
@@ -313,7 +335,7 @@
                 up_pass(0, 0, s, c - 2)
 
         if s == 1:
-            up_pass(0, 1, 0, 2)
+            up_pass(0, 1, 0, 3)
 
     for slot in range(1, slot_count):
         @pl.loop(0, pairs)
@@ -325,9 +347,9 @@
                     for s in others:
                         up_pass(0, 0, s, 2 + j)
 
-                @pl.when(j % 2 == 0)
+                @pl.when(j == 2)
                 def _():
-                    up_pass(0, 1, 0, 3 + j // 2)
+                    up_pass(0, 1, 0, 4)
 
                 @pl.when(j % 2 == 1)
                 def _():
@@ -408,26 +430,59 @@
     for c in late:
         up_pass(1, joints[1], 0, c)
 
+    held = (first - 2, first - 1)
+    axis_bit = orders[0][joints[0]]
+    upper = partner[axis_bit][0]
+    high = upper == 1
+    holds = mb == upper * (1 << axis_bit[1])
+
+    def join_held():
+        up_deep(0, 0, held[-1], 2)
+        for c in held:
+            up_join(c)
+
+    settled = max(0, min(first, down_chunks - SENT))
+
+    def up_sent(o, c, steps):
+        for k in steps:
+            for s in range(n_tp if k < joints[o] else 1):
+                up_copy(o, k, s, c).wait_send()
+
     @pl.loop(2, down_chunks)
     def _(t):
         dn_share(t)
 
+        @pl.when((t == 4) & jnp.logical_not(holds))
+        def _():
+            join_held()
+
         prefix(t - LAG * mb)
-
-    held = (first - 2, first - 1)
-    high = partner[orders[0][joints[0]]][0] == 1
+        dn_copy(0, t).wait_send()
+        for k in range(1, n_dp_steps):
+            dn_copy(k, t - 2).wait_send()
+
+        @pl.when(t == 5)
+        def _():
+            for s in others:
+                lat_copy(s).wait_send()
+                for slot in range(slot_count):
+                    lg_copy(s, slot).wait_send()
+            for c in late:
+                up_sent(1, c, range(joints[1]))
+
+        @pl.when((t >= SENT) & (t < SENT + settled))
+        def _():
+            up_sent(0, t - SENT, range(joints[0]))
 
     @pl.loop(0, LAG * (n_mb - 1))
     def _(u):
-        @pl.when(high & (u == 2 * mb))
-        def _():
-            up_deep(0, 0, held[-1], 2)
-            for c in held:
-                up_join(c)
+        @pl.when(holds & high & (u == 2))
+        def _():
+            join_held()
 
         prefix(down_chunks + u - LAG * mb)
 
-    @pl.when(jnp.logical_not(high))
+    @pl.when(holds & jnp.logical_not(high))
     def _():
         up_deep(0, 0, held[-1], 2)
         for c in held:
@@ -436,7 +491,7 @@
             up_copy(0, joints[0], 0, c).wait_recv()
             up_copy(0, joints[0], 0, c).start()
 
-    @pl.when(high)
+    @pl.when(high | jnp.logical_not(holds))
     def _():
         for c in held:
             up_copy(0, joints[0], 0, c).wait_recv()
@@ -453,31 +508,28 @@
             up_pass(1, j, 0, c)
         up_write(1, c)
 
-    for s in others:
-        lat_copy(s).wait_send()
-        for slot in range(slot_count):
-            lg_copy(s, slot).wait_send()
-
-    def up_sent(o, c):
-        for k in range(last + 1):
-            for s in range(n_tp if k < joints[o] else 1):
-                up_copy(o, k, s, c).wait_send()
+    for c in range(settled, first):
+        up_sent(0, c, range(joints[0]))
 
     @pl.loop(0, first)
     def _(c):
-        up_sent(0, c)
+        up_sent(0, c, range(joints[0], last + 1))
 
     for c in late:
-        up_sent(1, c)
+        up_sent(1, c, range(joints[1], last + 1))
+
+    for c in range(2):
+        dn_copy(0, c).wait_send()
+        for k in range(1, n_dp_steps):
+            dn_copy(k, down_chunks - 1 - c).wait_send()
+
+    waited = down_chunks + LAG * (n_mb - 1) - LAG * mb - SENT
 
     @pl.loop(0, down_chunks)
     def _(c):
-        for k in range(n_dp_steps):
-            dn_copy(k, c).wait_send()
-
-        @pl.when(mb < n_mb - 1)
-        def _():
-            pre_copy(c).wait_send()
+        @pl.when((mb < n_mb - 1) & (c >= waited))
+        def _():
+            pre_sent(c)
 
 
 def local(sizes, hidden, latent, out_grad, up_weight, mb_tokens, slot_mb):
@@ -490,6 +542,7 @@
     down_chunks = next(n for n in (14, 7) if feature_part % (128 * n) == 0)
     down_width = feature_part // down_chunks
     ahead = 2 * down_chunks // 7
+    halves = 2 if down_width % 256 == 0 else 1
     dp_bits, mb_bits = bits_of(n_dp), bits_of(n_mb)
     bits = dp_bits + mb_bits
     up_rows = rank >> bits
@@ -514,7 +567,7 @@
         dma((n_tp - 1,)), dma((n_tp - 1,)), dma((n_tp - 1, slot_count)), dma((n_tp - 1, slot_count)),
         dma((bits, n_tp, UP_CHUNKS)), dma((bits, n_tp, UP_CHUNKS)),
         dma((dp_bits, down_chunks)), dma((dp_bits, down_chunks)),
-        dma((down_chunks,)), dma((down_chunks,)),
+        dma((down_chunks, halves)), dma((down_chunks, halves)),
     ]
     hbm = pl.BlockSpec(memory_space=pl.ANY)
     smem = pl.BlockSpec(memory_space=pltpu.SMEM)

time: 87.3 us -> 87.5 us (level)
  no operation moved by 1% of the time
where the time goes in v3:
time: 87.5 us; the launch traced here: 87.3 us
  Pallas kernels  84.4 us (96%)
  local copies, waits for them, and re-layouts  2.2 us (3%)
    pallas_call x1, Pallas kernels, local(): pl.pallas_call(functools.partial(kernel, sizes), out_shape=(pltpu.VMEM((u...  84.4 us
    unnamed x2, local copies, waits for them, and re-layouts  2.2 us

profile of v3, /device:TPU:28, one launch (start us, length us, event | category | flops | bytes accessed | tf_op | source)
XLA Modules:
  0.0 87.3 jit_solution(4607572243563623161)
XLA Ops:
  0.6 84.4 %shard_map.77 = (f32[32,8192]{1,0:T(8,128)S(1)}, f32[1,3584,128]{2,1,0:T(8,128)S(1)}) custom-call(bf16[1,2,512,3584]{3,2,1,0:T(8,128)(2,1)} %hidden.1, bf16[1,2,512,256]{3,2,1,0:T(8,128)(2,1)} %latent.1, bf16[1,2,512,8192]{3,2,1,0:T(8,128)(2,1)} %grad.1, bf16[512,8192]{1,0:T(8,128)(2,1)} %weight.1, s32[1,8]{1,0:T(1,128)} %tokens.1, s32[1,2]{1,0:T(1,128)} %slots.1), custom_call_target="tpu_custom_call" | custom-call | tf_op jit(solution)/shard_map/pallas_call | solution.py:575
  85.1 1.0 %copy.10 = f32[32,8192]{1,0:T(8,128)} copy(f32[32,8192]{1,0:T(8,128)S(1)} %get-tuple-element.2) | data formatting | bytes 2097152
  86.1 1.2 %copy.11 = f32[1,3584,128]{2,1,0:T(8,128)} copy(f32[1,3584,128]{2,1,0:T(8,128)S(1)} %get-tuple-element.3) | data formatting | bytes 3670016
